TPU v7x, 256 devices: a whole 4x4x8 slice. The times are simulated.
256 devices in a mesh: rep: 16 (over y, x), mp: 16 (over z, core).
Axes of the slice: x: 4, y: 4, z: 8, core: 2. Of those that a mesh axis runs over, the one named last changes fastest.
Arguments:
- acts: bfloat16 [4096, 512, 256], P('rep', 'mp'), may hold values from -40 to 40, as said below
- refresh: int32 [512], P(('mp', 'rep')), may hold values from 0 to 16, as said below
- damping: float32 [512], P(('mp', 'rep')), may hold values from 0.2 to 1
- old_inverse: bfloat16 [512, 256, 256], P(('mp', 'rep')), may hold values from -0.375 to 0.375
- grads: bfloat16 [1024, 512, 256], P('rep', 'mp'), may hold values from -6 to 6
Outputs:
- covariance: float32 [512, 256, 256], P(('mp', 'rep'))
- new_inverse: bfloat16 [512, 256, 256], P(('mp', 'rep'))
- precond: bfloat16 [1024, 512, 256], P('rep', 'mp')
Inputs may be any that keep to these rules, and one draw needn't show every extreme that they name: `acts`: entries are bfloat16 values of order one with unequal feature scales. Block g * 32 + 2 * r + q (q = 0 or 1) is the q-th block of group g at replica index r. A block is refreshed only by a group through the same r. For every r, each group refreshes exactly one block through r. Of the two blocks of a group at r, at most one is refreshed by another group, and then the other one by the group itself. In every draw some groups refresh a block of another group.
All inputs are finite; a program needn't handle non-finite values. Where the computation divides by a largest or mean magnitude, that divisor is 1e-20 or more.
Results may differ from a plain program's by a relative error of at most 0.009.
Values may be sent and summed in bfloat16 or wider, within the bound.
No kernel may reach another device: no remote copies, remote signals or barrier semaphores. Data moves between devices by JAX's collectives and lax.ppermute only.
A program may use at most 64 MiB of HBM per device.

v0:
```python
import jax
import jax.numpy as jnp
from jax import lax
from jax.experimental import pallas as pl
from jax.experimental.pallas import tpu as pltpu
from jax.sharding import PartitionSpec as P

ITERS = 5
SIDE = 4
F32 = jnp.float32
BF16 = jnp.bfloat16
VM = pl.BlockSpec(memory_space=pltpu.VMEM)
SM = pl.BlockSpec(memory_space=pltpu.SMEM)


def square_index(n):
    return (
        lax.broadcasted_iota(jnp.int32, (n, n), 0),
        lax.broadcasted_iota(jnp.int32, (n, n), 1),
    )


def lay_out(scr, value):
    for j in range(scr.shape[0]):
        scr[j] = value[:, j * 128 : (j + 1) * 128].astype(F32)


def every(scr, start, count, stride):
    planes = [scr[j, pl.ds(start, count, stride=stride), :] for j in range(scr.shape[0])]
    return jnp.concatenate(planes, axis=1).astype(BF16)


def near(x):
    return pltpu.with_memory_space_constraint(x, pltpu.VMEM)


def place():
    rep = lax.axis_index("rep")
    return rep // SIDE, rep % SIDE, lax.axis_index("mp") % 2


def holder(first, second):
    y, x, other = place()
    ty = lax.rem(y + jnp.where(other == 0, second, first), SIDE)
    tx = lax.rem(x + jnp.where(other == 0, first, second), SIDE)
    return ty, tx


def swapping(n):
    row, col = square_index(n * n)
    return jnp.where(col == ((row & 15) << 4) + (row >> 4), 1.0, 0.0).astype(BF16)


def spread_rows(grads):
    rows, blocks, width = grads.shape
    n = 16

    def kernel(g_ref, *refs):
        outs, scr = refs[:SIDE], refs[SIDE]
        swap = swapping(n)
        for i in range(blocks // n):
            for h in range(rows // n):
                part = g_ref[n * h : n * (h + 1), n * i : n * (i + 1), :].reshape(n * n, width)
                part = mul(swap, part).astype(BF16)
                for k in range(n):
                    where = (n * i + k) // 2
                    scr[where, pl.ds((k % 2) * rows + n * h, n), :] = part[k * n : (k + 1) * n]
        for k in range(SIDE):
            for m in range(SIDE):
                ty, tx = holder(k, m)
                outs[k][m] = scr[SIDE * ty + tx]

    return pl.pallas_call(
        kernel,
        out_shape=(pltpu.VMEM((SIDE, 2 * rows, width), BF16),) * SIDE,
        in_specs=[VM],
        out_specs=(VM,) * SIDE,
        scratch_shapes=[pltpu.VMEM((blocks // 2, 2 * rows, width), BF16)],
        compiler_params=pltpu.CompilerParams(vmem_limit_bytes=12 << 20),
        name="spread_rows",
    )(grads)


def transpose_pieces(pieces):
    count = len(pieces)

    def kernel(*refs):
        for k in range(count):
            for m in range(count):
                refs[count + m][k] = refs[k][m]

    return pl.pallas_call(
        kernel,
        out_shape=(pltpu.VMEM(pieces[0].shape, BF16),) * count,
        in_specs=[VM] * count,
        out_specs=(VM,) * count,
        compiler_params=pltpu.CompilerParams(vmem_limit_bytes=12 << 20),
        name="transpose_pieces",
    )(*[near(piece) for piece in pieces])


def merge_rows(received):
    count, twice, width = received.shape
    rows = twice // 2
    blocks = 2 * count
    n = 16

    def kernel(r_ref, o_ref):
        swap = swapping(n)
        for i in range(blocks // n):
            for h in range(rows // n):
                part = jnp.concatenate(
                    [
                        r_ref[(n * i + k) // 2, pl.ds((k % 2) * rows + n * h, n), :]
                        for k in range(n)
                    ],
                    axis=0,
                )
                part = mul(swap, part).astype(BF16).reshape(n, n, width)
                o_ref[n * h : n * (h + 1), n * i : n * (i + 1), :] = part

    return pl.pallas_call(
        kernel,
        out_shape=jax.ShapeDtypeStruct((rows, blocks, width), BF16),
        in_specs=[VM],
        out_specs=VM,
        compiler_params=pltpu.CompilerParams(vmem_limit_bytes=12 << 20),
        name="merge_rows",
    )(near(received))


def step_along(value, shift, first):
    pairs = []
    groups = lax.axis_size("mp")
    for y in range(SIDE):
        for x in range(SIDE):
            for g in range(groups):
                along_x = (g % 2 == 0) == first
                ty, tx = (y, (x + shift) % SIDE) if along_x else ((y + shift) % SIDE, x)
                pairs.append(((SIDE * y + x) * groups + g, (SIDE * ty + tx) * groups + g))
    return lax.ppermute(value, ("rep", "mp"), pairs)


def lay_grams(scr, shifts, outs, tokens):
    half = scr.shape[3]
    width = 2 * half
    row, col = square_index(half)
    top_row = lax.broadcasted_iota(jnp.int32, (8, half), 0)
    for k, out in zip(shifts, outs):
        for m in range(SIDE):
            ty, tx = holder(k, m)
            last = jnp.zeros((8, half), F32)
            for q in range(2):
                v = every(scr.at[ty], 2 * tx + q, tokens, 2 * SIDE)
                gram = lax.dot_general(v, v, (((0,), (0,)), ((), ())), preferred_element_type=F32)
                low = gram[half:, half:]
                tri = jnp.where(row >= col, gram[:half, :half], low)
                out[m, q * width : q * width + half] = tri.astype(BF16)
                out[m, q * width + half : (q + 1) * width] = gram[:half, half:].astype(BF16)
                diagonal = jnp.sum(jnp.where(row == col, low, 0.0), axis=0, keepdims=True)
                last = jnp.where(top_row == q, diagonal, last)
            out[m, 2 * width :] = last.astype(BF16)


def first_grams(acts, shifts):
    tokens, _, width = acts.shape
    chunk = 2 * SIDE

    def kernel(a_hbm, *refs):
        outs, (scr, stage, sems) = refs[: len(shifts)], refs[len(shifts) :]
        copies = [
            pltpu.make_async_copy(a_hbm.at[:, pl.ds(chunk * i, chunk), :], stage.at[i], sems.at[i])
            for i in range(SIDE)
        ]
        for copy in copies:
            copy.start()
        for i in range(SIDE):
            copies[i].wait()
            lay_out(scr.at[i], stage[i].reshape(tokens * chunk, width))
        lay_grams(scr, shifts, outs, tokens)

    return pl.pallas_call(
        kernel,
        out_shape=(pltpu.VMEM((SIDE, 2 * width + 8, width // 2), BF16),) * len(shifts)
        + (pltpu.VMEM((SIDE, width // 128, tokens * chunk, 128), F32),),
        in_specs=[pl.BlockSpec(memory_space=pltpu.HBM)],
        out_specs=(VM,) * (len(shifts) + 1),
        scratch_shapes=[
            pltpu.VMEM((SIDE, tokens, chunk, width), BF16),
            pltpu.SemaphoreType.DMA((SIDE,)),
        ],
        compiler_params=pltpu.CompilerParams(vmem_limit_bytes=24 << 20),
        name="first_grams",
    )(pltpu.with_memory_space_constraint(acts, pltpu.HBM))


def other_grams(laid, shifts):
    half = laid.shape[3]
    tokens = laid.shape[2] // (2 * SIDE)

    def kernel(scr, *outs):
        lay_grams(scr, shifts, outs, tokens)

    return pl.pallas_call(
        kernel,
        out_shape=(pltpu.VMEM((SIDE, 4 * half + 8, half), BF16),) * len(shifts),
        in_specs=[VM],
        out_specs=(VM,) * len(shifts),
        compiler_params=pltpu.CompilerParams(vmem_limit_bytes=16 << 20),
        name="other_grams",
    )(near(laid))


def add_up(pieces):
    count, rows, half = pieces[0].shape

    def kernel(*refs):
        ins, outs = refs[: len(pieces)], refs[len(pieces) :]
        for m in range(count):
            total = ins[0][m].astype(F32)
            for ref in ins[1:]:
                total = total + ref[m].astype(F32)
            outs[m][...] = total.astype(outs[m].dtype)

    return pl.pallas_call(
        kernel,
        out_shape=(jax.ShapeDtypeStruct((rows, half), F32),)
        + (pltpu.VMEM((rows, half), BF16),) * (count - 1),
        in_specs=[VM] * len(pieces),
        out_specs=(VM,) * count,
        compiler_params=pltpu.CompilerParams(vmem_limit_bytes=12 << 20),
        name="add_up",
    )(*[near(piece) for piece in pieces])


def split(x):
    high = x.astype(BF16)
    return high, (x - high.astype(F32)).astype(BF16)


def mul(a, b):
    return lax.dot_general(a, b, (((1,), (0,)), ((), ())), preferred_element_type=F32)


def unpack(total, q, half):
    width = 2 * half
    row, col = square_index(half)
    tri = total[q * width : q * width + half]
    tri_t = tri.T
    cross = total[q * width + half : (q + 1) * width]
    diagonal = total[2 * width + q : 2 * width + q + 1]
    top = jnp.where(row >= col, tri, tri_t)
    low = jnp.where(row < col, tri, jnp.where(row > col, tri_t, diagonal))
    return jnp.concatenate(
        [jnp.concatenate([top, cross], axis=1), jnp.concatenate([cross.T, low], axis=1)], axis=0
    )


def refresh_blocks(pieces, damping, refresh, old_inverse, groups, tokens_all):
    slots, width, _ = old_inverse.shape
    half = width // 2

    def kernel(*refs):
        p_refs = refs[: len(pieces)]
        damp_ref, refresh_ref, old_ref, cov_ref, inv_ref, use_ref = refs[len(pieces) :]
        row, col = square_index(width)
        eye = jnp.where(row == col, 1.0, 0.0).astype(F32)
        total = p_refs[0][...].astype(F32)
        for ref in p_refs[1:]:
            total = total + ref[...].astype(F32)
        total = total * (1.0 / tokens_all)
        state = []
        for q in range(slots):
            cov = unpack(total, q, half)
            cov_ref[q] = cov
            matrix = cov + damp_ref[q] * eye
            bound = jnp.max(jnp.sum(jnp.abs(matrix), axis=0, keepdims=True), axis=1, keepdims=True)
            inv_bound = 1.0 / bound
            error = eye - matrix * inv_bound
            state.append((error, eye + error, inv_bound))
        for step in range(ITERS):
            following = []
            for error, series, inv_bound in state:
                e_high, e_low = split(error)
                if step == 0:
                    power = mul(e_high, e_high) + (mul(e_low, e_high) + mul(e_high, e_low))
                    following.append((power, series, inv_bound))
                    continue
                s_high, s_low = split(series)
                grown = mul(s_high, e_high) + (mul(s_low, e_high) + mul(s_high, e_low))
                power = error
                if step < ITERS - 1:
                    power = mul(e_high, e_high) + (mul(e_low, e_high) + mul(e_high, e_low))
                following.append((power, series + grown, inv_bound))
            state = following
        for q in range(slots):
            _, series, inv_bound = state[q]
            fresh = (series * inv_bound).astype(BF16)
            keep = (jnp.zeros((width, width), jnp.int32) + refresh_ref[q]) == groups
            inverse = jnp.where(keep, old_ref[q].astype(F32), fresh.astype(F32)).astype(BF16)
            inv_ref[q] = inverse
            use_ref[q] = inverse

    return pl.pallas_call(
        kernel,
        out_shape=(
            jax.ShapeDtypeStruct((slots, width, width), F32),
            jax.ShapeDtypeStruct((slots, width, width), BF16),
            pltpu.VMEM((slots, width, width), BF16),
        ),
        in_specs=[VM] * len(pieces) + [SM, SM, VM],
        out_specs=(VM,) * 3,
        compiler_params=pltpu.CompilerParams(vmem_limit_bytes=12 << 20),
        name="refresh_blocks",
    )(*[near(piece) for piece in pieces], damping, refresh, old_inverse)


def apply_inverse(pieces, inverse):
    _, twice, width = pieces[0].shape
    share = twice // 2

    def kernel(*refs):
        ins, (i_ref, o_ref) = refs[:SIDE], refs[SIDE:]
        for m in range(SIDE):
            for k in range(SIDE):
                ty, tx = holder(SIDE - k, SIDE - m)
                for q in range(2):
                    part = pl.ds(q * share, share)
                    o_ref[SIDE * ty + tx, part, :] = mul(ins[m][k, part, :], i_ref[q]).astype(BF16)

    return pl.pallas_call(
        kernel,
        out_shape=pltpu.VMEM((SIDE * SIDE, twice, width), BF16),
        in_specs=[VM] * (SIDE + 1),
        out_specs=VM,
        compiler_params=pltpu.CompilerParams(vmem_limit_bytes=12 << 20),
        name="apply_inverse",
    )(*[near(piece) for piece in pieces], near(inverse))


def ring(pieces, first, sign):
    moved = [pieces[0]]
    for k in range(1, SIDE):
        moved.append(step_along(pieces[k], (sign * k) % SIDE, first))
    return moved


def body(acts, refresh, damping, old_inverse, grads):
    replicas = lax.axis_size("rep")
    groups = lax.axis_size("mp")
    tokens_all = acts.shape[0] * replicas
    away, laid = first_grams(acts, (2,))
    ahead, behind, own = other_grams(laid, (1, 3, 0))
    pieces = ring((own, ahead, away, behind), True, 1)
    rows = spread_rows(grads)
    rows = ring(rows, True, 1)
    pieces = add_up(pieces)
    pieces = ring(pieces, False, 1)
    rows = transpose_pieces(rows)
    rows = ring(rows, False, 1)
    covariance, new_inverse, inverse = refresh_blocks(
        pieces, damping, refresh, old_inverse, groups, tokens_all
    )
    out = apply_inverse(rows, inverse)
    precond = merge_rows(lax.all_to_all(out, "rep", split_axis=0, concat_axis=0, tiled=True))
    return (covariance, new_inverse, precond)


def solution(mesh):
    return jax.shard_map(
        body,
        mesh=mesh,
        in_specs=(
            P("rep", "mp", None),
            P(("mp", "rep")),
            P(("mp", "rep")),
            P(("mp", "rep"), None, None),
            P("rep", "mp", None),
        ),
        out_specs=(
            P(("mp", "rep"), None, None),
            P(("mp", "rep"), None, None),
            P("rep", "mp", None),
        ),
        check_vma=False,
    )
```

profile of v0, /device:TPU:32, one launch (start us, length us, event | category | flops | bytes accessed | tf_op | source)
XLA Modules:
  0.0 68.8 jit_solution(16770732513685416643)
XLA Ops:
  0.7 3.1 %first_grams.1 = (bf16[4,520,128]{2,1,0:T(8,128)(2,1)S(1)}, f32[4,2,2048,128]{3,2,1,0:T(8,128)S(1)}) custom-call(bf16[256,32,256]{2,1,0:T(8,128)(2,1)} %a_hbm.1), custom_call_target="tpu_custom_call" | custom-call | tf_op jit(solution)/shard_map/first_grams/pallas_call | solution.py:182
  3.8 1.6 %other_grams.1 = (bf16[4,520,128]{2,1,0:T(8,128)(2,1)S(1)}, bf16[4,520,128]{2,1,0:T(8,128)(2,1)S(1)}, bf16[4,520,128]{2,1,0:T(8,128)(2,1)S(1)}) custom-call(f32[4,2,2048,128]{3,2,1,0:T(8,128)S(1)} %get-tuple-element.23.scr), custom_call_target="tpu_custom_call" | custom-call | tf_op jit(solution)/shard_map/other_grams/pallas_call | solution.py:204
  5.3 1.6 %collective-permute-start = (bf16[4,520,128]{2,1,0:T(8,128)(2,1)S(1)}, bf16[4,520,128]{2,1,0:T(8,128)(2,1)S(1)}, u32[]{:S(2)}, u32[]{:S(2)}) collective-permute-start(bf16[4,520,128]{2,1,0:T(8,128)(2,1)S(1)} %get-tuple-element.25), channel_id=1, source_target_pairs={{0,16},{1,65},{2,18},{3,67},{4,20},{5,69},{6,22},{7,71},{8,24},{9,... | collective-permute-start | bytes 1597448 | tf_op jit(solution)/shard_map/ppermute | solution.py:141
  6.9 1.7 %collective-permute-start.2 = (bf16[4,520,128]{2,1,0:T(8,128)(2,1)S(1)}, bf16[4,520,128]{2,1,0:T(8,128)(2,1)S(1)}, u32[]{:S(2)}, u32[]{:S(2)}) collective-permute-start(bf16[4,520,128]{2,1,0:T(8,128)(2,1)S(1)} %get-tuple-element.27), channel_id=1, source_target_pairs={{0,48},{1,193},{2,50},{3,195},{4,52},{5,197},{6,54},{7,199},{8,56}... | collective-permute-start | bytes 1597448 | tf_op jit(solution)/shard_map/ppermute | solution.py:141
  8.7 1.8 %collective-permute-start.1 = (bf16[4,520,128]{2,1,0:T(8,128)(2,1)S(1)}, bf16[4,520,128]{2,1,0:T(8,128)(2,1)S(1)}, u32[]{:S(2)}, u32[]{:S(2)}) collective-permute-start(bf16[4,520,128]{2,1,0:T(8,128)(2,1)S(1)} %get-tuple-element.26), channel_id=1, source_target_pairs={{0,32},{1,129},{2,34},{3,131},{4,36},{5,133},{6,38},{7,135},{8,40}... | collective-permute-start | bytes 1597448 | tf_op jit(solution)/shard_map/ppermute | solution.py:141
  10.5 0.5 spread_rows.1
  11.0 0.7 collective-permute-start.6
  11.7 2.0 %collective-permute-start.7 = (bf16[4,128,256]{2,1,0:T(8,128)(2,1)S(1)}, bf16[4,128,256]{2,1,0:T(8,128)(2,1)S(1)}, u32[]{:S(2)}, u32[]{:S(2)}) collective-permute-start(bf16[4,128,256]{2,1,0:T(8,128)(2,1)S(1)} %get-tuple-element.36), channel_id=1, source_target_pairs={{0,32},{1,129},{2,34},{3,131},{4,36},{5,133},{6,38},{7,135},{8,40}... | collective-permute-start | bytes 786440 | tf_op jit(solution)/shard_map/ppermute | solution.py:141
  13.7 2.2 %collective-permute-done.refs_1_ = bf16[4,520,128]{2,1,0:T(8,128)(2,1)S(1)} collective-permute-done((bf16[4,520,128]{2,1,0:T(8,128)(2,1)S(1)}, bf16[4,520,128]{2,1,0:T(8,128)(2,1)S(1)}, u32[]{:S(2)}, u32[]{:S(2)}) %collective-permute-start) | collective-permute-done | bytes 532512 | tf_op jit(solution)/shard_map/ppermute | solution.py:141
  15.9 1.5 %collective-permute-start.8 = (bf16[4,128,256]{2,1,0:T(8,128)(2,1)S(1)}, bf16[4,128,256]{2,1,0:T(8,128)(2,1)S(1)}, u32[]{:S(2)}, u32[]{:S(2)}) collective-permute-start(bf16[4,128,256]{2,1,0:T(8,128)(2,1)S(1)} %get-tuple-element.37), channel_id=1, source_target_pairs={{0,48},{1,193},{2,50},{3,195},{4,52},{5,197},{6,54},{7,199},{8,56}... | collective-permute-start | bytes 786440 | tf_op jit(solution)/shard_map/ppermute | solution.py:141
  17.4 6.5 %collective-permute-done.2.refs_3_ = bf16[4,520,128]{2,1,0:T(8,128)(2,1)S(1)} collective-permute-done((bf16[4,520,128]{2,1,0:T(8,128)(2,1)S(1)}, bf16[4,520,128]{2,1,0:T(8,128)(2,1)S(1)}, u32[]{:S(2)}, u32[]{:S(2)}) %collective-permute-start.2) | collective-permute-done | bytes 532512 | tf_op jit(solution)/shard_map/ppermute | solution.py:141
  24.3 1.7 %collective-permute-start.3 = (bf16[520,128]{1,0:T(8,128)(2,1)S(1)}, bf16[520,128]{1,0:T(8,128)(2,1)S(1)}, u32[]{:S(2)}, u32[]{:S(2)}) collective-permute-start(bf16[520,128]{1,0:T(8,128)(2,1)S(1)} %get-tuple-element.29), channel_id=1, source_target_pairs={{0,64},{1,17},{2,66},{3,19},{4,68},{5,21},{6,70},{7,23},{8,72},{9,... | collective-permute-start | bytes 399368 | tf_op jit(solution)/shard_map/ppermute | solution.py:141
  25.9 2.6 %collective-permute-done.7.refs_2_ = bf16[4,128,256]{2,1,0:T(8,128)(2,1)S(1)} collective-permute-done((bf16[4,128,256]{2,1,0:T(8,128)(2,1)S(1)}, bf16[4,128,256]{2,1,0:T(8,128)(2,1)S(1)}, u32[]{:S(2)}, u32[]{:S(2)}) %collective-permute-start.7) | collective-permute-done | bytes 262176 | tf_op jit(solution)/shard_map/ppermute | solution.py:141
  28.6 4.4 %collective-permute-start.10 = (bf16[4,128,256]{2,1,0:T(8,128)(2,1)S(1)}, bf16[4,128,256]{2,1,0:T(8,128)(2,1)S(1)}, u32[]{:S(2)}, u32[]{:S(2)}) collective-permute-start(bf16[4,128,256]{2,1,0:T(8,128)(2,1)S(1)} %get-tuple-element.40), channel_id=1, source_target_pairs={{0,128},{1,33},{2,130},{3,35},{4,132},{5,37},{6,134},{7,39},{8,136... | collective-permute-start | bytes 786440 | tf_op jit(solution)/shard_map/ppermute | solution.py:141
  33.0 1.1 %collective-permute-start.11 = (bf16[4,128,256]{2,1,0:T(8,128)(2,1)S(1)}, bf16[4,128,256]{2,1,0:T(8,128)(2,1)S(1)}, u32[]{:S(2)}, u32[]{:S(2)}) collective-permute-start(bf16[4,128,256]{2,1,0:T(8,128)(2,1)S(1)} %get-tuple-element.41), channel_id=1, source_target_pairs={{0,192},{1,49},{2,194},{3,51},{4,196},{5,53},{6,198},{7,55},{8,200... | collective-permute-start | bytes 786440 | tf_op jit(solution)/shard_map/ppermute | solution.py:141
  34.1 1.0 %collective-permute-start.9 = (bf16[4,128,256]{2,1,0:T(8,128)(2,1)S(1)}, bf16[4,128,256]{2,1,0:T(8,128)(2,1)S(1)}, u32[]{:S(2)}, u32[]{:S(2)}) collective-permute-start(bf16[4,128,256]{2,1,0:T(8,128)(2,1)S(1)} %get-tuple-element.39), channel_id=1, source_target_pairs={{0,64},{1,17},{2,66},{3,19},{4,68},{5,21},{6,70},{7,23},{8,72},{9,... | collective-permute-start | bytes 786440 | tf_op jit(solution)/shard_map/ppermute | solution.py:141
  35.1 0.5 collective-permute-start.4
  35.6 2.2 %collective-permute-start.5 = (bf16[520,128]{1,0:T(8,128)(2,1)S(1)}, bf16[520,128]{1,0:T(8,128)(2,1)S(1)}, u32[]{:S(2)}, u32[]{:S(2)}) collective-permute-start(bf16[520,128]{1,0:T(8,128)(2,1)S(1)} %get-tuple-element.31), channel_id=1, source_target_pairs={{0,192},{1,49},{2,194},{3,51},{4,196},{5,53},{6,198},{7,55},{8,200... | collective-permute-start | bytes 399368 | tf_op jit(solution)/shard_map/ppermute | solution.py:141
  37.7 4.0 %collective-permute-done.4.refs_2_ = bf16[520,128]{1,0:T(8,128)(2,1)S(1)} collective-permute-done((bf16[520,128]{1,0:T(8,128)(2,1)S(1)}, bf16[520,128]{1,0:T(8,128)(2,1)S(1)}, u32[]{:S(2)}, u32[]{:S(2)}) %collective-permute-start.4) | collective-permute-done | bytes 133152 | tf_op jit(solution)/shard_map/ppermute | solution.py:141
  41.7 0.9 %collective-permute-done.5.refs_3_ = bf16[520,128]{1,0:T(8,128)(2,1)S(1)} collective-permute-done((bf16[520,128]{1,0:T(8,128)(2,1)S(1)}, bf16[520,128]{1,0:T(8,128)(2,1)S(1)}, u32[]{:S(2)}, u32[]{:S(2)}) %collective-permute-start.5) | collective-permute-done | bytes 133152 | tf_op jit(solution)/shard_map/ppermute | solution.py:141
  42.6 3.6 %refresh_blocks.1 = (f32[2,256,256]{2,1,0:T(8,128)}, bf16[2,256,256]{2,1,0:T(8,128)(2,1)}, bf16[2,256,256]{2,1,0:T(8,128)(2,1)S(1)}) custom-call(f32[520,128]{1,0:T(8,128)S(1)} %get-tuple-element.28.refs_0_, bf16[520,128]{1,0:T(8,128)(2,1)S(1)} %collective-permute-done.3.refs_1_, bf16[520,128]{1,0:T(8,128)(2,1)S(1)} %collective-permute-done.4.refs_2_, ...), custom_call_target="tpu_custom_call" | custom-call | tf_op jit(solution)/shard_map/refresh_blocks/pallas_call | solution.py:304
  46.2 0.9 %apply_inverse.1 = bf16[16,128,256]{2,1,0:T(8,128)(2,1)S(1)} custom-call(bf16[4,128,256]{2,1,0:T(8,128)(2,1)S(1)} %get-tuple-element.38.refs_0_, bf16[4,128,256]{2,1,0:T(8,128)(2,1)S(1)} %collective-permute-done.9.refs_1_, bf16[4,128,256]{2,1,0:T(8,128)(2,1)S(1)} %collective-permute-done.10.refs_2_, ...), custom_call_target="tpu_custom_call" | custom-call | tf_op jit(solution)/shard_map/apply_inverse/pallas_call | solution.py:331
  47.0 20.4 %all_to_all.5.r_ref = bf16[16,128,256]{2,1,0:T(8,128)(2,1)S(1)} all-to-all(bf16[16,128,256]{2,1,0:T(8,128)(2,1)S(1)} %apply_inverse.1), channel_id=1, replica_groups=mesh['rep'=16,'mp'=16] {'rep'}, dimensions={0} | all-to-all | bytes 2097152 | tf_op jit(solution)/shard_map/all_to_all | solution.py:365
  67.4 1.4 %merge_rows.1 = bf16[64,32,256]{2,1,0:T(8,128)(2,1)} custom-call(bf16[16,128,256]{2,1,0:T(8,128)(2,1)S(1)} %all_to_all.5.r_ref), custom_call_target="tpu_custom_call" | custom-call | tf_op jit(solution)/shard_map/merge_rows/pallas_call | solution.py:122
  (17 shorter events, 0.4 us)
Async XLA Ops:
  0.6 9.8 %copy-start = (bf16[64,32,256]{2,1,0:T(8,128)(2,1)S(1)}, bf16[64,32,256]{2,1,0:T(8,128)(2,1)}, u32[]{:S(2)}) copy-start(bf16[64,32,256]{2,1,0:T(8,128)(2,1)} %g_ref.1) | copy-start | bytes 3145732
  0.6 41.9 %copy-start.3 = (s32[2]{0:T(128)S(1)}, s32[2]{0:T(128)}, u32[]{:S(2)}) copy-start(s32[2]{0:T(128)} %refs_5_.1) | copy-start | bytes 28
  0.7 41.9 %copy-start.2 = (f32[2]{0:T(128)S(1)}, f32[2]{0:T(128)}, u32[]{:S(2)}) copy-start(f32[2]{0:T(128)} %refs_4_.1) | copy-start | bytes 28
  0.7 41.9 %copy-start.1 = (bf16[2,256,256]{2,1,0:T(8,128)(2,1)S(1)}, bf16[2,256,256]{2,1,0:T(8,128)(2,1)}, u32[]{:S(2)}) copy-start(bf16[2,256,256]{2,1,0:T(8,128)(2,1)} %refs_6_.1) | copy-start | bytes 786436
  5.3 10.6 %collective-permute-start = (bf16[4,520,128]{2,1,0:T(8,128)(2,1)S(1)}, bf16[4,520,128]{2,1,0:T(8,128)(2,1)S(1)}, u32[]{:S(2)}, u32[]{:S(2)}) collective-permute-start(bf16[4,520,128]{2,1,0:T(8,128)(2,1)S(1)} %get-tuple-element.25), channel_id=1, source_target_pairs={{0,16},{1,65},{2,18},{3,67},{4,20},{5,69},{6,22},{7,71},{8,24},{9,... | collective-permute-start | bytes 1597448 | tf_op jit(solution)/shard_map/ppermute | solution.py:141
  6.9 17.1 %collective-permute-start.2 = (bf16[4,520,128]{2,1,0:T(8,128)(2,1)S(1)}, bf16[4,520,128]{2,1,0:T(8,128)(2,1)S(1)}, u32[]{:S(2)}, u32[]{:S(2)}) collective-permute-start(bf16[4,520,128]{2,1,0:T(8,128)(2,1)S(1)} %get-tuple-element.27), channel_id=1, source_target_pairs={{0,48},{1,193},{2,50},{3,195},{4,52},{5,197},{6,54},{7,199},{8,56}... | collective-permute-start | bytes 1597448 | tf_op jit(solution)/shard_map/ppermute | solution.py:141
  8.7 15.3 %collective-permute-start.1 = (bf16[4,520,128]{2,1,0:T(8,128)(2,1)S(1)}, bf16[4,520,128]{2,1,0:T(8,128)(2,1)S(1)}, u32[]{:S(2)}, u32[]{:S(2)}) collective-permute-start(bf16[4,520,128]{2,1,0:T(8,128)(2,1)S(1)} %get-tuple-element.26), channel_id=1, source_target_pairs={{0,32},{1,129},{2,34},{3,131},{4,36},{5,133},{6,38},{7,135},{8,40}... | collective-permute-start | bytes 1597448 | tf_op jit(solution)/shard_map/ppermute | solution.py:141
  11.0 14.9 %collective-permute-start.6 = (bf16[4,128,256]{2,1,0:T(8,128)(2,1)S(1)}, bf16[4,128,256]{2,1,0:T(8,128)(2,1)S(1)}, u32[]{:S(2)}, u32[]{:S(2)}) collective-permute-start(bf16[4,128,256]{2,1,0:T(8,128)(2,1)S(1)} %get-tuple-element.35), channel_id=1, source_target_pairs={{0,16},{1,65},{2,18},{3,67},{4,20},{5,69},{6,22},{7,71},{8,24},{9,... | collective-permute-start | bytes 786440 | tf_op jit(solution)/shard_map/ppermute | solution.py:141
  11.7 16.9 %collective-permute-start.7 = (bf16[4,128,256]{2,1,0:T(8,128)(2,1)S(1)}, bf16[4,128,256]{2,1,0:T(8,128)(2,1)S(1)}, u32[]{:S(2)}, u32[]{:S(2)}) collective-permute-start(bf16[4,128,256]{2,1,0:T(8,128)(2,1)S(1)} %get-tuple-element.36), channel_id=1, source_target_pairs={{0,32},{1,129},{2,34},{3,131},{4,36},{5,133},{6,38},{7,135},{8,40}... | collective-permute-start | bytes 786440 | tf_op jit(solution)/shard_map/ppermute | solution.py:141
  15.9 12.7 %collective-permute-start.8 = (bf16[4,128,256]{2,1,0:T(8,128)(2,1)S(1)}, bf16[4,128,256]{2,1,0:T(8,128)(2,1)S(1)}, u32[]{:S(2)}, u32[]{:S(2)}) collective-permute-start(bf16[4,128,256]{2,1,0:T(8,128)(2,1)S(1)} %get-tuple-element.37), channel_id=1, source_target_pairs={{0,48},{1,193},{2,50},{3,195},{4,52},{5,197},{6,54},{7,199},{8,56}... | collective-permute-start | bytes 786440 | tf_op jit(solution)/shard_map/ppermute | solution.py:141
  24.3 11.3 %collective-permute-start.3 = (bf16[520,128]{1,0:T(8,128)(2,1)S(1)}, bf16[520,128]{1,0:T(8,128)(2,1)S(1)}, u32[]{:S(2)}, u32[]{:S(2)}) collective-permute-start(bf16[520,128]{1,0:T(8,128)(2,1)S(1)} %get-tuple-element.29), channel_id=1, source_target_pairs={{0,64},{1,17},{2,66},{3,19},{4,68},{5,21},{6,70},{7,23},{8,72},{9,... | collective-permute-start | bytes 399368 | tf_op jit(solution)/shard_map/ppermute | solution.py:141
  28.6 17.5 %collective-permute-start.10 = (bf16[4,128,256]{2,1,0:T(8,128)(2,1)S(1)}, bf16[4,128,256]{2,1,0:T(8,128)(2,1)S(1)}, u32[]{:S(2)}, u32[]{:S(2)}) collective-permute-start(bf16[4,128,256]{2,1,0:T(8,128)(2,1)S(1)} %get-tuple-element.40), channel_id=1, source_target_pairs={{0,128},{1,33},{2,130},{3,35},{4,132},{5,37},{6,134},{7,39},{8,136... | collective-permute-start | bytes 786440 | tf_op jit(solution)/shard_map/ppermute | solution.py:141
  33.0 13.1 %collective-permute-start.11 = (bf16[4,128,256]{2,1,0:T(8,128)(2,1)S(1)}, bf16[4,128,256]{2,1,0:T(8,128)(2,1)S(1)}, u32[]{:S(2)}, u32[]{:S(2)}) collective-permute-start(bf16[4,128,256]{2,1,0:T(8,128)(2,1)S(1)} %get-tuple-element.41), channel_id=1, source_target_pairs={{0,192},{1,49},{2,194},{3,51},{4,196},{5,53},{6,198},{7,55},{8,200... | collective-permute-start | bytes 786440 | tf_op jit(solution)/shard_map/ppermute | solution.py:141
  34.1 12.1 %collective-permute-start.9 = (bf16[4,128,256]{2,1,0:T(8,128)(2,1)S(1)}, bf16[4,128,256]{2,1,0:T(8,128)(2,1)S(1)}, u32[]{:S(2)}, u32[]{:S(2)}) collective-permute-start(bf16[4,128,256]{2,1,0:T(8,128)(2,1)S(1)} %get-tuple-element.39), channel_id=1, source_target_pairs={{0,64},{1,17},{2,66},{3,19},{4,68},{5,21},{6,70},{7,23},{8,72},{9,... | collective-permute-start | bytes 786440 | tf_op jit(solution)/shard_map/ppermute | solution.py:141
  35.1 6.7 %collective-permute-start.4 = (bf16[520,128]{1,0:T(8,128)(2,1)S(1)}, bf16[520,128]{1,0:T(8,128)(2,1)S(1)}, u32[]{:S(2)}, u32[]{:S(2)}) collective-permute-start(bf16[520,128]{1,0:T(8,128)(2,1)S(1)} %get-tuple-element.30), channel_id=1, source_target_pairs={{0,128},{1,33},{2,130},{3,35},{4,132},{5,37},{6,134},{7,39},{8,136... | collective-permute-start | bytes 399368 | tf_op jit(solution)/shard_map/ppermute | solution.py:141
  35.6 7.0 %collective-permute-start.5 = (bf16[520,128]{1,0:T(8,128)(2,1)S(1)}, bf16[520,128]{1,0:T(8,128)(2,1)S(1)}, u32[]{:S(2)}, u32[]{:S(2)}) collective-permute-start(bf16[520,128]{1,0:T(8,128)(2,1)S(1)} %get-tuple-element.31), channel_id=1, source_target_pairs={{0,192},{1,49},{2,194},{3,51},{4,196},{5,53},{6,198},{7,55},{8,200... | collective-permute-start | bytes 399368 | tf_op jit(solution)/shard_map/ppermute | solution.py:141
where the time goes:
time: 68.9 us; the launch traced here: 68.8 us
  blocking collectives  20.4 us (30%)
  starting transfers between devices  20.1 us (29%)
  waiting for transfers between devices  16.3 us (24%)
  Pallas kernels  11.3 us (16%)
  between operations  0.72 us (1%)
    all_to_all x1, blocking collectives, body(): lax.all_to_all(out, 'rep', split_axis=0, concat_axis=0, tiled=True)  20.4 us
    ppermute x12, starting transfers between devices, step_along(): return lax.ppermute(value, ('rep', 'mp'), pairs)  20.1 us
    ppermute x12, waiting for transfers between devices, step_along(): return lax.ppermute(value, ('rep', 'mp'), pairs)  16.3 us
    pallas_call x1, Pallas kernels, refresh_blocks(): pl.pallas_call(kernel, out_shape=(jax.ShapeDtypeStruct((slots, width, wid...  3.57 us
    pallas_call x1, Pallas kernels, first_grams(): pl.pallas_call(kernel, out_shape=(pltpu.VMEM((SIDE, 2 * width + 8, width...  3.09 us
    pallas_call x1, Pallas kernels, other_grams(): pl.pallas_call(kernel, out_shape=(pltpu.VMEM((SIDE, 4 * half + 8, half),...  1.57 us
    pallas_call x1, Pallas kernels, merge_rows(): pl.pallas_call(kernel, out_shape=jax.ShapeDtypeStruct((rows, blocks, widt...  1.41 us
  transfers between devices with their start and end apart: 12, of which 5 were waited for; matrix products, arithmetic and copies ran while one was open for 0% of the time, Pallas kernels for 6%

commit v1 on v0

--- a/solution.py
+++ b/solution.py
@@ -7,6 +7,7 @@
 
 ITERS = 5
 SIDE = 4
+FINE = 3
 F32 = jnp.float32
 BF16 = jnp.bfloat16
 VM = pl.BlockSpec(memory_space=pltpu.VMEM)
@@ -81,37 +82,24 @@
     )(grads)
 
 
-def transpose_pieces(pieces):
-    count = len(pieces)
+def merge_rows(pieces):
+    _, twice, width = pieces[0].shape
+    rows = twice // 2
+    blocks = 2 * SIDE * SIDE
+    n = 16
 
     def kernel(*refs):
-        for k in range(count):
-            for m in range(count):
-                refs[count + m][k] = refs[k][m]
-
-    return pl.pallas_call(
-        kernel,
-        out_shape=(pltpu.VMEM(pieces[0].shape, BF16),) * count,
-        in_specs=[VM] * count,
-        out_specs=(VM,) * count,
-        compiler_params=pltpu.CompilerParams(vmem_limit_bytes=12 << 20),
-        name="transpose_pieces",
-    )(*[near(piece) for piece in pieces])
-
-
-def merge_rows(received):
-    count, twice, width = received.shape
-    rows = twice // 2
-    blocks = 2 * count
-    n = 16
-
-    def kernel(r_ref, o_ref):
+        ins, (o_ref, scr) = refs[:SIDE], refs[SIDE:]
         swap = swapping(n)
+        for k in range(SIDE):
+            for m in range(SIDE):
+                ty, tx = holder(k, m)
+                scr[SIDE * ty + tx] = ins[k][m]
         for i in range(blocks // n):
             for h in range(rows // n):
                 part = jnp.concatenate(
                     [
-                        r_ref[(n * i + k) // 2, pl.ds((k % 2) * rows + n * h, n), :]
+                        scr[(n * i + k) // 2, pl.ds((k % 2) * rows + n * h, n), :]
                         for k in range(n)
                     ],
                     axis=0,
@@ -122,11 +110,12 @@
     return pl.pallas_call(
         kernel,
         out_shape=jax.ShapeDtypeStruct((rows, blocks, width), BF16),
-        in_specs=[VM],
+        in_specs=[VM] * SIDE,
         out_specs=VM,
+        scratch_shapes=[pltpu.VMEM((blocks // 2, twice, width), BF16)],
         compiler_params=pltpu.CompilerParams(vmem_limit_bytes=12 << 20),
         name="merge_rows",
-    )(near(received))
+    )(*[near(piece) for piece in pieces])
 
 
 def step_along(value, shift, first):
@@ -224,7 +213,7 @@
 
     return pl.pallas_call(
         kernel,
-        out_shape=(jax.ShapeDtypeStruct((rows, half), F32),)
+        out_shape=(pltpu.VMEM((rows, half), F32),)
         + (pltpu.VMEM((rows, half), BF16),) * (count - 1),
         in_specs=[VM] * len(pieces),
         out_specs=(VM,) * count,
@@ -240,6 +229,12 @@
 
 def mul(a, b):
     return lax.dot_general(a, b, (((1,), (0,)), ((), ())), preferred_element_type=F32)
+
+
+def times(a, b, fine):
+    if not fine:
+        return mul(a[0], b[0])
+    return mul(a[0], b[0]) + (mul(a[1], b[0]) + mul(a[0], b[1]))
 
 
 def unpack(total, q, half):
@@ -262,7 +257,7 @@
 
     def kernel(*refs):
         p_refs = refs[: len(pieces)]
-        damp_ref, refresh_ref, old_ref, cov_ref, inv_ref, use_ref = refs[len(pieces) :]
+        damp_ref, refresh_ref, old_ref, cov_ref, inv_ref = refs[len(pieces) :]
         row, col = square_index(width)
         eye = jnp.where(row == col, 1.0, 0.0).astype(F32)
         total = p_refs[0][...].astype(F32)
@@ -279,19 +274,16 @@
             error = eye - matrix * inv_bound
             state.append((error, eye + error, inv_bound))
         for step in range(ITERS):
+            fine = step < FINE
             following = []
             for error, series, inv_bound in state:
-                e_high, e_low = split(error)
-                if step == 0:
-                    power = mul(e_high, e_high) + (mul(e_low, e_high) + mul(e_high, e_low))
-                    following.append((power, series, inv_bound))
-                    continue
-                s_high, s_low = split(series)
-                grown = mul(s_high, e_high) + (mul(s_low, e_high) + mul(s_high, e_low))
+                e_parts = split(error)
                 power = error
+                if step > 0:
+                    series = series + times(split(series), e_parts, fine)
                 if step < ITERS - 1:
-                    power = mul(e_high, e_high) + (mul(e_low, e_high) + mul(e_high, e_low))
-                following.append((power, series + grown, inv_bound))
+                    power = times(e_parts, e_parts, fine)
+                following.append((power, series, inv_bound))
             state = following
         for q in range(slots):
             _, series, inv_bound = state[q]
@@ -299,43 +291,42 @@
             keep = (jnp.zeros((width, width), jnp.int32) + refresh_ref[q]) == groups
             inverse = jnp.where(keep, old_ref[q].astype(F32), fresh.astype(F32)).astype(BF16)
             inv_ref[q] = inverse
-            use_ref[q] = inverse
 
     return pl.pallas_call(
         kernel,
         out_shape=(
-            jax.ShapeDtypeStruct((slots, width, width), F32),
-            jax.ShapeDtypeStruct((slots, width, width), BF16),
+            pltpu.VMEM((slots, width, width), F32),
             pltpu.VMEM((slots, width, width), BF16),
         ),
         in_specs=[VM] * len(pieces) + [SM, SM, VM],
-        out_specs=(VM,) * 3,
+        out_specs=(VM,) * 2,
         compiler_params=pltpu.CompilerParams(vmem_limit_bytes=12 << 20),
         name="refresh_blocks",
     )(*[near(piece) for piece in pieces], damping, refresh, old_inverse)
 
 
-def apply_inverse(pieces, inverse):
+def apply_inverses(pieces, inverses):
     _, twice, width = pieces[0].shape
     share = twice // 2
 
     def kernel(*refs):
-        ins, (i_ref, o_ref) = refs[:SIDE], refs[SIDE:]
+        ins, invs, outs = refs[:SIDE], refs[SIDE : 2 * SIDE], refs[2 * SIDE :]
         for m in range(SIDE):
-            for k in range(SIDE):
-                ty, tx = holder(SIDE - k, SIDE - m)
-                for q in range(2):
-                    part = pl.ds(q * share, share)
-                    o_ref[SIDE * ty + tx, part, :] = mul(ins[m][k, part, :], i_ref[q]).astype(BF16)
-
-    return pl.pallas_call(
-        kernel,
-        out_shape=pltpu.VMEM((SIDE * SIDE, twice, width), BF16),
-        in_specs=[VM] * (SIDE + 1),
-        out_specs=VM,
-        compiler_params=pltpu.CompilerParams(vmem_limit_bytes=12 << 20),
-        name="apply_inverse",
-    )(*[near(piece) for piece in pieces], near(inverse))
+            for q in range(2):
+                part = pl.ds(q * share, share)
+                flat = jnp.concatenate([ref[m, part, :] for ref in ins], axis=0)
+                out = mul(flat, invs[m][q]).astype(BF16)
+                for k in range(SIDE):
+                    outs[k][m, part, :] = out[k * share : (k + 1) * share]
+
+    return pl.pallas_call(
+        kernel,
+        out_shape=(pltpu.VMEM((SIDE, twice, width), BF16),) * SIDE,
+        in_specs=[VM] * (2 * SIDE),
+        out_specs=(VM,) * SIDE,
+        compiler_params=pltpu.CompilerParams(vmem_limit_bytes=12 << 20),
+        name="apply_inverses",
+    )(*[near(piece) for piece in pieces], *[near(inverse) for inverse in inverses])
 
 
 def ring(pieces, first, sign):
@@ -356,14 +347,12 @@
     rows = ring(rows, True, 1)
     pieces = add_up(pieces)
     pieces = ring(pieces, False, 1)
-    rows = transpose_pieces(rows)
-    rows = ring(rows, False, 1)
-    covariance, new_inverse, inverse = refresh_blocks(
-        pieces, damping, refresh, old_inverse, groups, tokens_all
-    )
-    out = apply_inverse(rows, inverse)
-    precond = merge_rows(lax.all_to_all(out, "rep", split_axis=0, concat_axis=0, tiled=True))
-    return (covariance, new_inverse, precond)
+    covariance, inverse = refresh_blocks(pieces, damping, refresh, old_inverse, groups, tokens_all)
+    inverses = ring((inverse,) * SIDE, False, -1)
+    out = apply_inverses(rows, inverses)
+    out = ring(out, True, -1)
+    precond = merge_rows(out)
+    return (covariance, inverse, precond)
 
 
 def solution(mesh):

time: 68.9 us -> 65.9 us (0.956)
  the two profiles are of different devices: /device:TPU:32 before, /device:TPU:8 now
where the time goes in v1:
time: 65.9 us
  waiting for transfers between devices  32.9 us (50%)
  starting transfers between devices  20.8 us (32%)
  Pallas kernels  9.92 us (15%)
  local copies, waits for them, and re-layouts  1.51 us (2%)
  between operations  0.72 us (1%)
    ppermute x15, waiting for transfers between devices, step_along(): return lax.ppermute(value, ('rep', 'mp'), pairs)  32.9 us
    ppermute x15, starting transfers between devices, step_along(): return lax.ppermute(value, ('rep', 'mp'), pairs)  20.8 us
    pallas_call x1, Pallas kernels, first_grams(): pl.pallas_call(kernel, out_shape=(pltpu.VMEM((SIDE, 2 * width + 8, width...  3.09 us
    pallas_call x1, Pallas kernels, refresh_blocks(): pl.pallas_call(kernel, out_shape=(pltpu.VMEM((slots, width, width), F32),...  2.53 us
    pallas_call x1, Pallas kernels, other_grams(): pl.pallas_call(kernel, out_shape=(pltpu.VMEM((SIDE, 4 * half + 8, half),...  1.57 us
    pallas_call x1, Pallas kernels, merge_rows(): pl.pallas_call(kernel, out_shape=jax.ShapeDtypeStruct((rows, blocks, widt...  1.52 us
    unnamed x10, local copies, waits for them, and re-layouts  1.51 us
  transfers between devices with their start and end apart: 15, of which 10 were waited for; matrix products, arithmetic and copies ran while one was open for 2% of the time, Pallas kernels for 5%

profile of v1, /device:TPU:8, one launch (start us, length us, event | category | flops | bytes accessed | tf_op | source)
XLA Modules:
  0.0 65.9 jit_solution(10787889240643216739)
XLA Ops:
  0.7 3.1 %first_grams.1 = (bf16[4,520,128]{2,1,0:T(8,128)(2,1)S(1)}, f32[4,2,2048,128]{3,2,1,0:T(8,128)S(1)}) custom-call(bf16[256,32,256]{2,1,0:T(8,128)(2,1)} %a_hbm.1), custom_call_target="tpu_custom_call" | custom-call | tf_op jit(solution)/shard_map/first_grams/pallas_call | solution.py:171
  3.8 1.6 %other_grams.1 = (bf16[4,520,128]{2,1,0:T(8,128)(2,1)S(1)}, bf16[4,520,128]{2,1,0:T(8,128)(2,1)S(1)}, bf16[4,520,128]{2,1,0:T(8,128)(2,1)S(1)}) custom-call(f32[4,2,2048,128]{3,2,1,0:T(8,128)S(1)} %get-tuple-element.22.scr), custom_call_target="tpu_custom_call" | custom-call | tf_op jit(solution)/shard_map/other_grams/pallas_call | solution.py:193
  5.3 1.6 %collective-permute-start = (bf16[4,520,128]{2,1,0:T(8,128)(2,1)S(1)}, bf16[4,520,128]{2,1,0:T(8,128)(2,1)S(1)}, u32[]{:S(2)}, u32[]{:S(2)}) collective-permute-start(bf16[4,520,128]{2,1,0:T(8,128)(2,1)S(1)} %get-tuple-element.24), channel_id=1, source_target_pairs={{0,16},{1,65},{2,18},{3,67},{4,20},{5,69},{6,22},{7,71},{8,24},{9,... | collective-permute-start | bytes 1597448 | tf_op jit(solution)/shard_map/ppermute | solution.py:130
  6.9 1.7 %collective-permute-start.2 = (bf16[4,520,128]{2,1,0:T(8,128)(2,1)S(1)}, bf16[4,520,128]{2,1,0:T(8,128)(2,1)S(1)}, u32[]{:S(2)}, u32[]{:S(2)}) collective-permute-start(bf16[4,520,128]{2,1,0:T(8,128)(2,1)S(1)} %get-tuple-element.26), channel_id=1, source_target_pairs={{0,48},{1,193},{2,50},{3,195},{4,52},{5,197},{6,54},{7,199},{8,56}... | collective-permute-start | bytes 1597448 | tf_op jit(solution)/shard_map/ppermute | solution.py:130
  8.7 1.8 %collective-permute-start.1 = (bf16[4,520,128]{2,1,0:T(8,128)(2,1)S(1)}, bf16[4,520,128]{2,1,0:T(8,128)(2,1)S(1)}, u32[]{:S(2)}, u32[]{:S(2)}) collective-permute-start(bf16[4,520,128]{2,1,0:T(8,128)(2,1)S(1)} %get-tuple-element.25), channel_id=1, source_target_pairs={{0,32},{1,129},{2,34},{3,131},{4,36},{5,133},{6,38},{7,135},{8,40}... | collective-permute-start | bytes 1597448 | tf_op jit(solution)/shard_map/ppermute | solution.py:130
  11.7 4.2 %collective-permute-done.refs_1_ = bf16[4,520,128]{2,1,0:T(8,128)(2,1)S(1)} collective-permute-done((bf16[4,520,128]{2,1,0:T(8,128)(2,1)S(1)}, bf16[4,520,128]{2,1,0:T(8,128)(2,1)S(1)}, u32[]{:S(2)}, u32[]{:S(2)}) %collective-permute-start) | collective-permute-done | bytes 532512 | tf_op jit(solution)/shard_map/ppermute | solution.py:130
  15.9 5.3 %collective-permute-done.2.refs_3_ = bf16[4,520,128]{2,1,0:T(8,128)(2,1)S(1)} collective-permute-done((bf16[4,520,128]{2,1,0:T(8,128)(2,1)S(1)}, bf16[4,520,128]{2,1,0:T(8,128)(2,1)S(1)}, u32[]{:S(2)}, u32[]{:S(2)}) %collective-permute-start.2) | collective-permute-done | bytes 532512 | tf_op jit(solution)/shard_map/ppermute | solution.py:130
  21.2 1.5 %collective-permute-done.1.refs_2_ = bf16[4,520,128]{2,1,0:T(8,128)(2,1)S(1)} collective-permute-done((bf16[4,520,128]{2,1,0:T(8,128)(2,1)S(1)}, bf16[4,520,128]{2,1,0:T(8,128)(2,1)S(1)}, u32[]{:S(2)}, u32[]{:S(2)}) %collective-permute-start.1) | collective-permute-done | bytes 532512 | tf_op jit(solution)/shard_map/ppermute | solution.py:130
  23.0 1.6 %collective-permute-start.3 = (bf16[520,128]{1,0:T(8,128)(2,1)S(1)}, bf16[520,128]{1,0:T(8,128)(2,1)S(1)}, u32[]{:S(2)}, u32[]{:S(2)}) collective-permute-start(bf16[520,128]{1,0:T(8,128)(2,1)S(1)} %get-tuple-element.28), channel_id=1, source_target_pairs={{0,64},{1,17},{2,66},{3,19},{4,68},{5,21},{6,70},{7,23},{8,72},{9,... | collective-permute-start | bytes 399368 | tf_op jit(solution)/shard_map/ppermute | solution.py:130
  24.6 1.6 %collective-permute-start.4 = (bf16[520,128]{1,0:T(8,128)(2,1)S(1)}, bf16[520,128]{1,0:T(8,128)(2,1)S(1)}, u32[]{:S(2)}, u32[]{:S(2)}) collective-permute-start(bf16[520,128]{1,0:T(8,128)(2,1)S(1)} %get-tuple-element.29), channel_id=1, source_target_pairs={{0,128},{1,33},{2,130},{3,35},{4,132},{5,37},{6,134},{7,39},{8,136... | collective-permute-start | bytes 399368 | tf_op jit(solution)/shard_map/ppermute | solution.py:130
  26.2 1.8 %collective-permute-start.5 = (bf16[520,128]{1,0:T(8,128)(2,1)S(1)}, bf16[520,128]{1,0:T(8,128)(2,1)S(1)}, u32[]{:S(2)}, u32[]{:S(2)}) collective-permute-start(bf16[520,128]{1,0:T(8,128)(2,1)S(1)} %get-tuple-element.30), channel_id=1, source_target_pairs={{0,192},{1,49},{2,194},{3,51},{4,196},{5,53},{6,198},{7,55},{8,200... | collective-permute-start | bytes 399368 | tf_op jit(solution)/shard_map/ppermute | solution.py:130
  28.0 0.8 %collective-permute-start.7 = (bf16[4,128,256]{2,1,0:T(8,128)(2,1)S(1)}, bf16[4,128,256]{2,1,0:T(8,128)(2,1)S(1)}, u32[]{:S(2)}, u32[]{:S(2)}) collective-permute-start(bf16[4,128,256]{2,1,0:T(8,128)(2,1)S(1)} %get-tuple-element.35), channel_id=1, source_target_pairs={{0,32},{1,129},{2,34},{3,131},{4,36},{5,133},{6,38},{7,135},{8,40}... | collective-permute-start | bytes 786440 | tf_op jit(solution)/shard_map/ppermute | solution.py:130
  28.8 3.2 %collective-permute-start.8 = (bf16[4,128,256]{2,1,0:T(8,128)(2,1)S(1)}, bf16[4,128,256]{2,1,0:T(8,128)(2,1)S(1)}, u32[]{:S(2)}, u32[]{:S(2)}) collective-permute-start(bf16[4,128,256]{2,1,0:T(8,128)(2,1)S(1)} %get-tuple-element.36), channel_id=1, source_target_pairs={{0,48},{1,193},{2,50},{3,195},{4,52},{5,197},{6,54},{7,199},{8,56}... | collective-permute-start | bytes 786440 | tf_op jit(solution)/shard_map/ppermute | solution.py:130
  32.0 4.8 %collective-permute-done.5.refs_3_ = bf16[520,128]{1,0:T(8,128)(2,1)S(1)} collective-permute-done((bf16[520,128]{1,0:T(8,128)(2,1)S(1)}, bf16[520,128]{1,0:T(8,128)(2,1)S(1)}, u32[]{:S(2)}, u32[]{:S(2)}) %collective-permute-start.5) | collective-permute-done | bytes 133152 | tf_op jit(solution)/shard_map/ppermute | solution.py:130
  36.7 2.5 %refresh_blocks.1 = (f32[2,256,256]{2,1,0:T(8,128)S(1)}, bf16[2,256,256]{2,1,0:T(8,128)(2,1)S(1)}) custom-call(f32[520,128]{1,0:T(8,128)S(1)} %get-tuple-element.27.refs_0_, bf16[520,128]{1,0:T(8,128)(2,1)S(1)} %collective-permute-done.3.refs_1_, bf16[520,128]{1,0:T(8,128)(2,1)S(1)} %collective-permute-done.4.refs_2_, ...), custom_call_target="tpu_custom_call" | custom-call | tf_op jit(solution)/shard_map/refresh_blocks/pallas_call | solution.py:295
  39.3 1.9 %collective-permute-start.10 = (bf16[2,256,256]{2,1,0:T(8,128)(2,1)S(1)}, bf16[2,256,256]{2,1,0:T(8,128)(2,1)S(1)}, u32[]{:S(2)}, u32[]{:S(2)}) collective-permute-start(bf16[2,256,256]{2,1,0:T(8,128)(2,1)S(1)} %get-tuple-element.42.refs_4_), channel_id=1, source_target_pairs={{0,128},{1,33},{2,130},{3,35},{4,132},{5,37},{6,134},{7,39},{8,136... | collective-permute-start | bytes 786440 | tf_op jit(solution)/shard_map/ppermute | solution.py:130
  41.8 1.3 %collective-permute-start.9 = (bf16[2,256,256]{2,1,0:T(8,128)(2,1)S(1)}, bf16[2,256,256]{2,1,0:T(8,128)(2,1)S(1)}, u32[]{:S(2)}, u32[]{:S(2)}) collective-permute-start(bf16[2,256,256]{2,1,0:T(8,128)(2,1)S(1)} %get-tuple-element.42.refs_4_), channel_id=1, source_target_pairs={{0,192},{1,49},{2,194},{3,51},{4,196},{5,53},{6,198},{7,55},{8,200... | collective-permute-start | bytes 786440 | tf_op jit(solution)/shard_map/ppermute | solution.py:130
  43.1 4.3 %collective-permute-done.10.refs_6_ = bf16[2,256,256]{2,1,0:T(8,128)(2,1)S(1)} collective-permute-done((bf16[2,256,256]{2,1,0:T(8,128)(2,1)S(1)}, bf16[2,256,256]{2,1,0:T(8,128)(2,1)S(1)}, u32[]{:S(2)}, u32[]{:S(2)}) %collective-permute-start.10) | collective-permute-done | bytes 262176 | tf_op jit(solution)/shard_map/ppermute | solution.py:130
  48.3 4.6 %collective-permute-done.9.refs_5_ = bf16[2,256,256]{2,1,0:T(8,128)(2,1)S(1)} collective-permute-done((bf16[2,256,256]{2,1,0:T(8,128)(2,1)S(1)}, bf16[2,256,256]{2,1,0:T(8,128)(2,1)S(1)}, u32[]{:S(2)}, u32[]{:S(2)}) %collective-permute-start.9) | collective-permute-done | bytes 262176 | tf_op jit(solution)/shard_map/ppermute | solution.py:130
  53.7 1.6 %collective-permute-start.13 = (bf16[4,128,256]{2,1,0:T(8,128)(2,1)S(1)}, bf16[4,128,256]{2,1,0:T(8,128)(2,1)S(1)}, u32[]{:S(2)}, u32[]{:S(2)}) collective-permute-start(bf16[4,128,256]{2,1,0:T(8,128)(2,1)S(1)} %get-tuple-element.39), channel_id=1, source_target_pairs={{0,32},{1,129},{2,34},{3,131},{4,36},{5,133},{6,38},{7,135},{8,40}... | collective-permute-start | bytes 786440 | tf_op jit(solution)/shard_map/ppermute | solution.py:130
  57.0 2.8 %collective-permute-done.12.refs_1_ = bf16[4,128,256]{2,1,0:T(8,128)(2,1)S(1)} collective-permute-done((bf16[4,128,256]{2,1,0:T(8,128)(2,1)S(1)}, bf16[4,128,256]{2,1,0:T(8,128)(2,1)S(1)}, u32[]{:S(2)}, u32[]{:S(2)}) %collective-permute-start.12) | collective-permute-done | bytes 262176 | tf_op jit(solution)/shard_map/ppermute | solution.py:130
  59.8 1.8 %collective-permute-done.13.refs_2_ = bf16[4,128,256]{2,1,0:T(8,128)(2,1)S(1)} collective-permute-done((bf16[4,128,256]{2,1,0:T(8,128)(2,1)S(1)}, bf16[4,128,256]{2,1,0:T(8,128)(2,1)S(1)}, u32[]{:S(2)}, u32[]{:S(2)}) %collective-permute-start.13) | collective-permute-done | bytes 262176 | tf_op jit(solution)/shard_map/ppermute | solution.py:130
  61.6 2.7 %collective-permute-done.14.refs_3_ = bf16[4,128,256]{2,1,0:T(8,128)(2,1)S(1)} collective-permute-done((bf16[4,128,256]{2,1,0:T(8,128)(2,1)S(1)}, bf16[4,128,256]{2,1,0:T(8,128)(2,1)S(1)}, u32[]{:S(2)}, u32[]{:S(2)}) %collective-permute-start.14) | collective-permute-done | bytes 262176 | tf_op jit(solution)/shard_map/ppermute | solution.py:130
  64.3 1.5 %merge_rows.1 = bf16[64,32,256]{2,1,0:T(8,128)(2,1)} custom-call(bf16[4,128,256]{2,1,0:T(8,128)(2,1)S(1)} %get-tuple-element.37.refs_0_, bf16[4,128,256]{2,1,0:T(8,128)(2,1)S(1)} %collective-permute-done.12.refs_1_, bf16[4,128,256]{2,1,0:T(8,128)(2,1)S(1)} %collective-permute-done.13.refs_2_, bf16[4,128,256]{2,1,0:T(8,128)(2,1)S(1)} %collective-permute-done.14.refs_3_), custom_call_target="tpu_custom_call" | custom-call | tf_op jit(solution)/shard_map/merge_rows/pallas_call | solution.py:110
  (23 shorter events, 5.4 us)
Async XLA Ops:
  0.6 9.8 %copy-start = (bf16[64,32,256]{2,1,0:T(8,128)(2,1)S(1)}, bf16[64,32,256]{2,1,0:T(8,128)(2,1)}, u32[]{:S(2)}) copy-start(bf16[64,32,256]{2,1,0:T(8,128)(2,1)} %g_ref.1) | copy-start | bytes 3145732
  0.6 36.1 %copy-start.3 = (s32[2]{0:T(128)S(1)}, s32[2]{0:T(128)}, u32[]{:S(2)}) copy-start(s32[2]{0:T(128)} %refs_5_.1) | copy-start | bytes 28
  0.7 36.1 %copy-start.2 = (f32[2]{0:T(128)S(1)}, f32[2]{0:T(128)}, u32[]{:S(2)}) copy-start(f32[2]{0:T(128)} %refs_4_.1) | copy-start | bytes 28
  0.7 36.1 %copy-start.1 = (bf16[2,256,256]{2,1,0:T(8,128)(2,1)S(1)}, bf16[2,256,256]{2,1,0:T(8,128)(2,1)}, u32[]{:S(2)}) copy-start(bf16[2,256,256]{2,1,0:T(8,128)(2,1)} %refs_6_.1) | copy-start | bytes 786436
  5.3 10.6 %collective-permute-start = (bf16[4,520,128]{2,1,0:T(8,128)(2,1)S(1)}, bf16[4,520,128]{2,1,0:T(8,128)(2,1)S(1)}, u32[]{:S(2)}, u32[]{:S(2)}) collective-permute-start(bf16[4,520,128]{2,1,0:T(8,128)(2,1)S(1)} %get-tuple-element.24), channel_id=1, source_target_pairs={{0,16},{1,65},{2,18},{3,67},{4,20},{5,69},{6,22},{7,71},{8,24},{9,... | collective-permute-start | bytes 1597448 | tf_op jit(solution)/shard_map/ppermute | solution.py:130
  6.9 14.3 %collective-permute-start.2 = (bf16[4,520,128]{2,1,0:T(8,128)(2,1)S(1)}, bf16[4,520,128]{2,1,0:T(8,128)(2,1)S(1)}, u32[]{:S(2)}, u32[]{:S(2)}) collective-permute-start(bf16[4,520,128]{2,1,0:T(8,128)(2,1)S(1)} %get-tuple-element.26), channel_id=1, source_target_pairs={{0,48},{1,193},{2,50},{3,195},{4,52},{5,197},{6,54},{7,199},{8,56}... | collective-permute-start | bytes 1597448 | tf_op jit(solution)/shard_map/ppermute | solution.py:130
  8.7 14.0 %collective-permute-start.1 = (bf16[4,520,128]{2,1,0:T(8,128)(2,1)S(1)}, bf16[4,520,128]{2,1,0:T(8,128)(2,1)S(1)}, u32[]{:S(2)}, u32[]{:S(2)}) collective-permute-start(bf16[4,520,128]{2,1,0:T(8,128)(2,1)S(1)} %get-tuple-element.25), channel_id=1, source_target_pairs={{0,32},{1,129},{2,34},{3,131},{4,36},{5,133},{6,38},{7,135},{8,40}... | collective-permute-start | bytes 1597448 | tf_op jit(solution)/shard_map/ppermute | solution.py:130
  11.0 30.8 %collective-permute-start.6 = (bf16[4,128,256]{2,1,0:T(8,128)(2,1)S(1)}, bf16[4,128,256]{2,1,0:T(8,128)(2,1)S(1)}, u32[]{:S(2)}, u32[]{:S(2)}) collective-permute-start(bf16[4,128,256]{2,1,0:T(8,128)(2,1)S(1)} %get-tuple-element.34), channel_id=1, source_target_pairs={{0,16},{1,65},{2,18},{3,67},{4,20},{5,69},{6,22},{7,71},{8,24},{9,... | collective-permute-start | bytes 786440 | tf_op jit(solution)/shard_map/ppermute | solution.py:130
  23.0 5.8 %collective-permute-start.3 = (bf16[520,128]{1,0:T(8,128)(2,1)S(1)}, bf16[520,128]{1,0:T(8,128)(2,1)S(1)}, u32[]{:S(2)}, u32[]{:S(2)}) collective-permute-start(bf16[520,128]{1,0:T(8,128)(2,1)S(1)} %get-tuple-element.28), channel_id=1, source_target_pairs={{0,64},{1,17},{2,66},{3,19},{4,68},{5,21},{6,70},{7,23},{8,72},{9,... | collective-permute-start | bytes 399368 | tf_op jit(solution)/shard_map/ppermute | solution.py:130
  24.6 7.4 %collective-permute-start.4 = (bf16[520,128]{1,0:T(8,128)(2,1)S(1)}, bf16[520,128]{1,0:T(8,128)(2,1)S(1)}, u32[]{:S(2)}, u32[]{:S(2)}) collective-permute-start(bf16[520,128]{1,0:T(8,128)(2,1)S(1)} %get-tuple-element.29), channel_id=1, source_target_pairs={{0,128},{1,33},{2,130},{3,35},{4,132},{5,37},{6,134},{7,39},{8,136... | collective-permute-start | bytes 399368 | tf_op jit(solution)/shard_map/ppermute | solution.py:130
  26.2 10.5 %collective-permute-start.5 = (bf16[520,128]{1,0:T(8,128)(2,1)S(1)}, bf16[520,128]{1,0:T(8,128)(2,1)S(1)}, u32[]{:S(2)}, u32[]{:S(2)}) collective-permute-start(bf16[520,128]{1,0:T(8,128)(2,1)S(1)} %get-tuple-element.30), channel_id=1, source_target_pairs={{0,192},{1,49},{2,194},{3,51},{4,196},{5,53},{6,198},{7,55},{8,200... | collective-permute-start | bytes 399368 | tf_op jit(solution)/shard_map/ppermute | solution.py:130
  28.0 15.2 %collective-permute-start.7 = (bf16[4,128,256]{2,1,0:T(8,128)(2,1)S(1)}, bf16[4,128,256]{2,1,0:T(8,128)(2,1)S(1)}, u32[]{:S(2)}, u32[]{:S(2)}) collective-permute-start(bf16[4,128,256]{2,1,0:T(8,128)(2,1)S(1)} %get-tuple-element.35), channel_id=1, source_target_pairs={{0,32},{1,129},{2,34},{3,131},{4,36},{5,133},{6,38},{7,135},{8,40}... | collective-permute-start | bytes 786440 | tf_op jit(solution)/shard_map/ppermute | solution.py:130
  28.8 14.4 %collective-permute-start.8 = (bf16[4,128,256]{2,1,0:T(8,128)(2,1)S(1)}, bf16[4,128,256]{2,1,0:T(8,128)(2,1)S(1)}, u32[]{:S(2)}, u32[]{:S(2)}) collective-permute-start(bf16[4,128,256]{2,1,0:T(8,128)(2,1)S(1)} %get-tuple-element.36), channel_id=1, source_target_pairs={{0,48},{1,193},{2,50},{3,195},{4,52},{5,197},{6,54},{7,199},{8,56}... | collective-permute-start | bytes 786440 | tf_op jit(solution)/shard_map/ppermute | solution.py:130
  39.3 8.2 %collective-permute-start.10 = (bf16[2,256,256]{2,1,0:T(8,128)(2,1)S(1)}, bf16[2,256,256]{2,1,0:T(8,128)(2,1)S(1)}, u32[]{:S(2)}, u32[]{:S(2)}) collective-permute-start(bf16[2,256,256]{2,1,0:T(8,128)(2,1)S(1)} %get-tuple-element.42.refs_4_), channel_id=1, source_target_pairs={{0,128},{1,33},{2,130},{3,35},{4,132},{5,37},{6,134},{7,39},{8,136... | collective-permute-start | bytes 786440 | tf_op jit(solution)/shard_map/ppermute | solution.py:130
  41.1 7.2 %collective-permute-start.11 = (bf16[2,256,256]{2,1,0:T(8,128)(2,1)S(1)}, bf16[2,256,256]{2,1,0:T(8,128)(2,1)S(1)}, u32[]{:S(2)}, u32[]{:S(2)}) collective-permute-start(bf16[2,256,256]{2,1,0:T(8,128)(2,1)S(1)} %get-tuple-element.42.refs_4_), channel_id=1, source_target_pairs={{0,64},{1,17},{2,66},{3,19},{4,68},{5,21},{6,70},{7,23},{8,72},{9,... | collective-permute-start | bytes 786440 | tf_op jit(solution)/shard_map/ppermute | solution.py:130
  41.8 11.1 %collective-permute-start.9 = (bf16[2,256,256]{2,1,0:T(8,128)(2,1)S(1)}, bf16[2,256,256]{2,1,0:T(8,128)(2,1)S(1)}, u32[]{:S(2)}, u32[]{:S(2)}) collective-permute-start(bf16[2,256,256]{2,1,0:T(8,128)(2,1)S(1)} %get-tuple-element.42.refs_4_), channel_id=1, source_target_pairs={{0,192},{1,49},{2,194},{3,51},{4,196},{5,53},{6,198},{7,55},{8,200... | collective-permute-start | bytes 786440 | tf_op jit(solution)/shard_map/ppermute | solution.py:130
  53.4 6.4 %collective-permute-start.12 = (bf16[4,128,256]{2,1,0:T(8,128)(2,1)S(1)}, bf16[4,128,256]{2,1,0:T(8,128)(2,1)S(1)}, u32[]{:S(2)}, u32[]{:S(2)}) collective-permute-start(bf16[4,128,256]{2,1,0:T(8,128)(2,1)S(1)} %get-tuple-element.38), channel_id=1, source_target_pairs={{0,48},{1,193},{2,50},{3,195},{4,52},{5,197},{6,54},{7,199},{8,56}... | collective-permute-start | bytes 786440 | tf_op jit(solution)/shard_map/ppermute | solution.py:130
  53.7 8.0 %collective-permute-start.13 = (bf16[4,128,256]{2,1,0:T(8,128)(2,1)S(1)}, bf16[4,128,256]{2,1,0:T(8,128)(2,1)S(1)}, u32[]{:S(2)}, u32[]{:S(2)}) collective-permute-start(bf16[4,128,256]{2,1,0:T(8,128)(2,1)S(1)} %get-tuple-element.39), channel_id=1, source_target_pairs={{0,32},{1,129},{2,34},{3,131},{4,36},{5,133},{6,38},{7,135},{8,40}... | collective-permute-start | bytes 786440 | tf_op jit(solution)/shard_map/ppermute | solution.py:130
  55.3 9.1 %collective-permute-start.14 = (bf16[4,128,256]{2,1,0:T(8,128)(2,1)S(1)}, bf16[4,128,256]{2,1,0:T(8,128)(2,1)S(1)}, u32[]{:S(2)}, u32[]{:S(2)}) collective-permute-start(bf16[4,128,256]{2,1,0:T(8,128)(2,1)S(1)} %get-tuple-element.40), channel_id=1, source_target_pairs={{0,16},{1,65},{2,18},{3,67},{4,20},{5,69},{6,22},{7,71},{8,24},{9,... | collective-permute-start | bytes 786440 | tf_op jit(solution)/shard_map/ppermute | solution.py:130
